TPU v7x, 32 devices: a whole 2x2x4 slice. The times are simulated.
32 devices in a mesh: ep: 4 (over y, core), fsdp: 8 (over z, x).
Axes of the slice: x: 2, y: 2, z: 4, core: 2. Of those that a mesh axis runs over, the one named last changes fastest.
Arguments:
- master_down: float32 [16, 6400, 4096], P('ep', None, 'fsdp'), may hold values from -0.109375 to 0.109375
- second_down: bfloat16 [16, 6400, 4096], P('ep', None, 'fsdp'), may hold values from -0.0390625 to 0.0390625
- router_weight: float32 [4096, 16], P('fsdp', 'ep'), may hold values from -0.09375 to 0.09375
- router_gain: float32 [4096], P('fsdp'), may hold values from 0.25 to 1.75
Outputs:
- final_down: bfloat16 [16, 6400, 4096], P('ep', 'fsdp')
- scale_down: float32 [16, 6400], P('ep', 'fsdp')
- serve_router: bfloat16 [4096, 16], replicated
All inputs are finite; a program needn't handle non-finite values.
Results may differ from a plain program's by a relative error of at most 0.001.
Values may be sent and summed in bfloat16 or wider, within the bound.
A program may use at most 256 MiB of HBM per device.

v0:
```python
import jax
import jax.numpy as jnp
from jax import lax
from jax.sharding import PartitionSpec as P


def shards(master_down, second_down, router_weight, router_gain):
    merged_down = master_down + second_down.astype(jnp.float32)
    total_down = lax.psum(jnp.sum(merged_down * merged_down, axis=2), "fsdp")
    scale_down = jnp.sqrt(total_down)
    narrow_down = (merged_down / jnp.expand_dims(scale_down, 2)).astype(jnp.bfloat16)
    final_down = lax.all_to_all(narrow_down, "fsdp", split_axis=1, concat_axis=2, tiled=True)
    scale_down = lax.dynamic_slice_in_dim(
        scale_down, lax.axis_index("fsdp") * final_down.shape[1], final_down.shape[1], axis=1
    )
    part_router = (router_weight * router_gain[:, None]).astype(jnp.bfloat16)
    row_router = lax.all_gather(part_router, "fsdp", axis=0, tiled=True)
    serve_router = lax.all_gather(row_router, "ep", axis=1, tiled=True)
    return (final_down, scale_down, serve_router)


def solution(mesh):
    return jax.shard_map(
        shards,
        mesh=mesh,
        in_specs=(P("ep", None, "fsdp"), P("ep", None, "fsdp"), P("fsdp", "ep"), P("fsdp")),
        out_specs=(P("ep", "fsdp", None), P("ep", "fsdp"), P()),
        check_vma=False,
    )
```

profile of v0, /device:TPU:0, one launch (start us, length us, event | category | flops | bytes accessed | tf_op | source)
XLA Modules:
  0.0 905.5 jit_solution(8188198296431997854)
XLA Ops:
  7.2 0.0 all-reduce.2.cloned.1.call-start
  7.2 24.2 %multiply_reduce_fusion = f32[4,6400]{1,0:T(4,128)S(1)} fusion(f32[4,6400,512]{2,1,0:T(8,128)} %param.4, bf16[4,6400,512]{2,1,0:T(8,128)(2,1)} %param.5), kind=kLoop, calls=%fused_computation.1 | loop fusion | flops 52403200 | bytes 78745600 | tf_op jit(solution)/shard_map/reduce_sum | solution.py:9
  31.4 2.3 copy.21
  33.7 0.0 all-reduce.2.cloned.1.call-update
  33.7 135.6 %all-reduce.2.cloned.1.call-done = f32[4,6400]{0,1:T(8,128)} async-done(((f32[4,6400]{0,1:T(8,128)}), f32[4,6400]{0,1:T(8,128)}) %all-reduce.2.cloned.1.call-update) | async-done | bytes 102416 | tf_op jit(solution)/shard_map/psum | solution.py:9
  169.3 2.7 sqrt.3
  172.0 1.2 copy.17
  173.3 34.3 %divide_convert_fusion = bf16[4,6400,512]{2,1,0:T(8,128)(2,1)} fusion(f32[4,6400,512]{2,1,0:T(8,128)} %param.4, bf16[4,6400,512]{2,1,0:T(8,128)(2,1)} %param.5, f32[4,6400]{1,0:T(4,128)S(1)} %copy.17), kind=kLoop, calls=%fused_computation | loop fusion | flops 52428800 | bytes 104960000 | tf_op jit(solution)/shard_map/convert_element_type | solution.py:11
  207.5 33.4 %copy.18 = bf16[4,6400,512]{2,0,1:T(4,128)(2,1)} copy(bf16[4,6400,512]{2,1,0:T(8,128)(2,1)} %divide_convert_fusion) | data formatting | bytes 52428800 | tf_op jit(solution)/shard_map/convert_element_type | solution.py:11
  240.9 0.0 copy-start
  240.9 0.0 copy-start.1
  240.9 6.6 all-to-all-start
  247.6 0.0 copy-done
  247.6 0.0 copy-done.1
  247.6 585.0 %all_gather.6 = bf16[4096,4]{0,1:T(4,128)(2,1)S(1)} all-gather(bf16[512,4]{0,1:T(4,128)(2,1)S(1)} %multiply_convert_fusion), channel_id=1, replica_groups=mesh['ep'=4,'fsdp'=8] {'fsdp'}, dimensions={0}, use_global_device_ids=true | all-gather | bytes 36864 | tf_op jit(solution)/shard_map/all_gather | solution.py:17
  832.7 5.4 all-gather
  838.1 0.7 reshape.9
  838.8 0.8 constant_dynamic-slice_fusion
  839.5 1.8 copy.20
  841.3 0.0 all-to-all-done
  841.3 18.2 %copy.19 = bf16[4,800,8,512]{3,2,1,0:T(8,128)(2,1)} copy(bf16[4,800,8,512]{3,0,1,2:T(4,128)(2,1)} %bitcast.1) | data formatting | bytes 52428800 | tf_op jit(solution)/shard_map/all_to_all | solution.py:12
  859.5 39.2 %all_to_all.16 = bf16[4,800,4096]{2,1,0:T(8,128)(2,1)} reshape(bf16[4,800,8,512]{3,2,1,0:T(8,128)(2,1)} %copy.19) | data formatting | bytes 52428800 | tf_op jit(solution)/shard_map/all_to_all | solution.py:12
  (1 shorter events, 0.0 us)
Async XLA Ops:
  7.2 162.2 %all-reduce.2.cloned.1.call-start = ((), (), s32[]{:S(2)}) async-start(), calls=%async_computation.1 | async-start | bytes 6553600 | tf_op jit(solution)/shard_map/psum | solution.py:9
  240.9 6.7 copy-start
  240.9 6.7 copy-start.1
  240.9 600.4 %all-to-all-start = ((bf16[4,6400,512]{2,0,1:T(4,128)(2,1)}), bf16[4,6400,512]{2,0,1:T(4,128)(2,1)}, u32[]{:S(2)}, u32[]{:S(2)}) async-start(bf16[4,6400,512]{2,0,1:T(4,128)(2,1)} %copy.18), calls=%async_computation | async-start | bytes 52428800 | tf_op jit(solution)/shard_map/all_to_all | solution.py:12
Sparse Core Ops, SparseCore 0:
  33.9 135.4 all-reduce.1
where the time goes:
time: 907 us; the launch traced here: 906 us
  blocking collectives  590 us (65%)
  waiting for transfers between devices  136 us (15%)
  local copies, waits for them, and re-layouts  100 us (11%)
  other arithmetic  58.5 us (6%)
  between operations  14.1 us (2%)
    all_gather x1, blocking collectives, shards(): row_router = lax.all_gather(part_router, 'fsdp', axis=0, tiled=True)  585 us
    psum x1, waiting for transfers between devices, shards(): total_down = lax.psum(jnp.sum(merged_down * merged_down, axis=2), 'fsdp')  136 us
    all_to_all x2, local copies, waits for them, and re-layouts, shards(): lax.all_to_all(narrow_down, 'fsdp', split_axis=1, concat_axis=2, tiled=True)  57.4 us
    convert_element_type x1, other arithmetic, shards(): (merged_down / jnp.expand_dims(scale_down, 2)).astype(jnp.bfloat16)  34.3 us
    convert_element_type x1, local copies, waits for them, and re-layouts, shards(): (merged_down / jnp.expand_dims(scale_down, 2)).astype(jnp.bfloat16)  33.4 us
    reduce_sum x1, other arithmetic, shards(): total_down = lax.psum(jnp.sum(merged_down * merged_down, axis=2), 'fsdp')  24.2 us
  transfers between devices with their start and end apart: 2, of which 1 were waited for; matrix products, arithmetic and copies ran while one was open for 0% of the time, Pallas kernels for 0%

commit v1 on v0

v1 whole, which is shorter than its diff:
```python
import functools

import jax
import jax.numpy as jnp
from jax import lax
from jax.experimental import pallas as pl
from jax.experimental.pallas import tpu as pltpu
from jax.sharding import PartitionSpec as P

MESH = pl.DeviceIdType.MESH
LANES = 128
RING = 4
SLOTS = 4


def largest_divisor(size, limit, step):
    return max(d for d in range(step, limit + 1, step) if size % d == 0)


def kernel(dims, master, second, router, gain, final, scales, routers,
           held, narrow, part, gathered, total, inverse, sent, router_part,
           master_sem, second_sem, part_send, part_recv, total_send, total_recv,
           block_send, block_own, block_recv, router_send, router_recv):
    groups, fsdp, experts, steps, rows, width, blocks, size = dims
    chunks = experts * steps
    me, group = lax.axis_index("fsdp"), lax.axis_index("ep")
    peers = [lax.rem(me + k, fsdp) for k in range(1, fsdp)]
    others = [lax.rem(group + k, groups) for k in range(1, groups)]

    def load(t):
        e, s = t // steps, t % steps
        span = pl.ds(pl.multiple_of(s * rows, 8), rows)
        return (
            pltpu.make_async_copy(master.at[e, :, span, :], held.at[t % RING], master_sem.at[t % RING]),
            pltpu.make_async_copy(second.at[e, :, span, :], narrow.at[t % 2], second_sem.at[t % 2]),
        )

    for t in range(min(2, chunks)):
        for copy in load(t):
            copy.start()

    barrier = pltpu.get_barrier_semaphore()
    for p in peers:
        pl.semaphore_signal(barrier, inc=1, device_id={"fsdp": p}, device_id_type=MESH)
    for g in others:
        pl.semaphore_signal(barrier, inc=1, device_id={"ep": g}, device_id_type=MESH)
    pl.semaphore_wait(barrier, len(peers) + len(others))

    def router_copy(p):
        return pltpu.make_async_remote_copy(
            router_part, routers.at[group, me], router_send.at[0], router_recv.at[0],
            device_id={"fsdp": p}, device_id_type=MESH)

    def router_rows(g):
        return pltpu.make_async_remote_copy(
            routers.at[group], routers.at[group], router_send.at[1], router_recv.at[1],
            device_id={"ep": g}, device_id_type=MESH)

    own_router = (router[...] * gain[...]).astype(jnp.bfloat16)
    router_part[...] = own_router
    routers[group, me] = own_router

    def stats(t):
        for copy in load(t):
            copy.wait()
        slot, side = t % RING, t % 2

        def body(d, _):
            for b in range(blocks):
                span = pl.ds(b * size, size)
                x = held[slot, d, span, :] + narrow[side, d, span, :].astype(jnp.float32)
                held[slot, d, span, :] = x
                x = x * x
                acc = x[:, :LANES]
                for c in range(LANES, width, LANES):
                    acc = acc + x[:, c:c + LANES]
                if size < LANES:
                    acc = jnp.concatenate([acc, jnp.zeros((LANES - size, LANES), jnp.float32)], axis=0)
                part[t, d, pl.ds(b, 1), :] = jnp.sum(acc.T, axis=0, keepdims=True)
            return 0

        lax.fori_loop(0, fsdp, body, 0)
        gathered[t, me] = part[t, me]
        for p in peers:
            pltpu.make_async_remote_copy(
                part.at[t, p], gathered.at[t, me], part_send.at[t], part_recv.at[t],
                device_id={"fsdp": p}, device_id_type=MESH).start()

    def many(ref, t, sem):
        seven = ref.at[t, pl.ds(0, fsdp - 1)]
        return pltpu.make_async_copy(seven, seven, sem)

    def reduce(t):
        many(gathered, t, part_recv.at[t]).wait()
        scale = jnp.sqrt(jnp.sum(gathered[t], axis=0))
        scales[t] = scale
        back = 1.0 / scale
        total[t] = back
        inverse[t, me] = back
        for p in peers:
            pltpu.make_async_remote_copy(
                total.at[t], inverse.at[t, me], total_send.at[t], total_recv.at[t],
                device_id={"fsdp": p}, device_id_type=MESH).start()

    def place(t):
        e, s = t // steps, t % steps
        return final.at[e, pl.ds(pl.multiple_of(s * rows, 8), rows), pl.ds(pl.multiple_of(me * width, LANES), width)]

    def own_copy(t):
        return pltpu.make_async_copy(sent.at[t % SLOTS, me], place(t), block_own.at[t % SLOTS])

    def drain(t):
        many(sent, t % SLOTS, block_send.at[t % SLOTS]).wait()
        own_copy(t).wait()

    def norm(t):
        many(inverse, t, total_recv.at[t]).wait()
        many(part, t, part_send.at[t]).wait()
        many(inverse, t, total_send.at[t]).wait()

        @pl.when(t >= SLOTS)
        def _():
            drain(t - SLOTS)

        slot, out = t % RING, t % SLOTS

        def body(d, _):
            for b in range(blocks):
                span = pl.ds(b * size, size)
                row = inverse[t, d, pl.ds(b, 1), :]
                factor = jnp.broadcast_to(row, (LANES, LANES)).T[:size]
                for c in range(0, width, LANES):
                    x = held[slot, d, span, c:c + LANES] * factor
                    sent[out, d, span, c:c + LANES] = x.astype(jnp.bfloat16)
            return 0

        lax.fori_loop(0, fsdp, body, 0)
        for p in peers:
            pltpu.make_async_remote_copy(
                sent.at[out, p], place(t), block_send.at[out], block_recv.at[me],
                device_id={"fsdp": p}, device_id_type=MESH).start()
        own_copy(t).start()

    def step(u, _):
        @pl.when(u < chunks)
        def _():
            stats(u)

        @pl.when((u >= 1) & (u < chunks + 1))
        def _():
            reduce(u - 1)

        @pl.when(u >= 2)
        def _():
            norm(u - 2)

        @pl.when(u + 2 < chunks)
        def _():
            for copy in load(u + 2):
                copy.start()

        return 0

    lax.fori_loop(0, chunks + 2, step, 0)

    for p in peers:
        router_copy(p).start()
    seven = routers.at[group, pl.ds(0, fsdp - 1)]
    pltpu.make_async_copy(seven, seven, router_send.at[0]).wait()
    pltpu.make_async_copy(seven, seven, router_recv.at[0]).wait()
    for g in others:
        router_rows(g).start()
    three = routers.at[pl.ds(0, groups - 1)]
    pltpu.make_async_copy(three, three, router_send.at[1]).wait()
    pltpu.make_async_copy(three, three, router_recv.at[1]).wait()

    def last(t, _):
        drain(t)
        return 0

    lax.fori_loop(max(0, chunks - SLOTS), chunks, last, 0)
    for p in peers:
        column = final.at[:, :, pl.ds(pl.multiple_of(p * width, LANES), width)]
        pltpu.make_async_copy(column, column, block_recv.at[p]).wait()


def solution(mesh):
    groups, fsdp = mesh.shape["ep"], mesh.shape["fsdp"]

    def step(master, second, router, gain):
        experts, height, width = master.shape
        own = height // fsdp
        rows = largest_divisor(own, 160, 8)
        size = largest_divisor(rows, LANES, 8)
        blocks, steps = rows // size, own // rows
        chunks = experts * steps
        dims = (groups, fsdp, experts, steps, rows, width, blocks, size)
        columns = router.shape[1]
        anywhere = pl.BlockSpec(memory_space=pl.ANY)
        inside = pl.BlockSpec(memory_space=pltpu.VMEM)
        tall = (chunks, fsdp, blocks, LANES)
        dma = pltpu.SemaphoreType.DMA
        final, scales, routers = pl.pallas_call(
            functools.partial(kernel, dims),
            out_shape=(
                jax.ShapeDtypeStruct((experts, own, fsdp * width), jnp.bfloat16),
                jax.ShapeDtypeStruct((chunks, blocks, LANES), jnp.float32),
                jax.ShapeDtypeStruct((groups, fsdp, columns, width), jnp.bfloat16),
            ),
            in_specs=[anywhere, anywhere, inside, inside],
            out_specs=(anywhere, inside, inside),
            scratch_shapes=[
                pltpu.VMEM((RING, fsdp, rows, width), jnp.float32),
                pltpu.VMEM((2, fsdp, rows, width), jnp.bfloat16),
                pltpu.VMEM(tall, jnp.float32),
                pltpu.VMEM(tall, jnp.float32),
                pltpu.VMEM((chunks, blocks, LANES), jnp.float32),
                pltpu.VMEM(tall, jnp.float32),
                pltpu.VMEM((SLOTS, fsdp, rows, width), jnp.bfloat16),
                pltpu.VMEM((columns, width), jnp.bfloat16),
                dma((RING,)), dma((2,)),
                dma((chunks,)), dma((chunks,)), dma((chunks,)), dma((chunks,)),
                dma((SLOTS,)), dma((SLOTS,)), dma((fsdp,)),
                dma((2,)), dma((2,)),
            ],
            compiler_params=pltpu.CompilerParams(
                collective_id=0, has_side_effects=True, vmem_limit_bytes=48 * 2**20),
        )(
            master.reshape(experts, fsdp, own, width),
            second.reshape(experts, fsdp, own, width),
            router.T,
            gain[None, :],
        )
        scale = scales[:, :, :size].reshape(experts, own)
        routers = routers.transpose(1, 3, 0, 2).reshape(fsdp * width, groups * columns)
        return final, scale, routers

    return jax.shard_map(
        step,
        mesh=mesh,
        in_specs=(P("ep", None, "fsdp"), P("ep", None, "fsdp"), P("fsdp", "ep"), P("fsdp")),
        out_specs=(P("ep", "fsdp", None), P("ep", "fsdp"), P()),
        check_vma=False,
    )
```

time: 907 us -> 612 us (0.67)
  Pallas kernels: 0 us -> 590 us
  blocking collectives: 590 us -> 0 us
  waiting for transfers between devices: 136 us -> 0 us
  local copies, waits for them, and re-layouts: 100 us -> 20.7 us
  other arithmetic: 58.5 us -> 0 us
  between operations: 14.1 us -> 0.65 us
    all_gather x2 -> x0, blocking collectives: 590 us -> none  [the longest x1 585 us: shards(): row_router = lax.all_gather(part_router, 'fsdp', axis=0, tiled=True)]
    pallas_call x0 -> x1, Pallas kernels: none -> 590 us  [step(): pl.pallas_call(functools.partial(kernel, dims), out_shape=(jax.ShapeDtype...]
    psum x1 -> x0, waiting for transfers between devices: 136 us -> none  [shards(): total_down = lax.psum(jnp.sum(merged_down * merged_down, axis=2), 'fsdp')]
    all_to_all x2 -> x0, local copies, waits for them, and re-layouts: 57.4 us -> none  [shards(): lax.all_to_all(narrow_down, 'fsdp', split_axis=1, concat_axis=2, tiled=True)]
    convert_element_type x2 -> x0, other arithmetic: 34.3 us -> none  [the longest x1 34.3 us: shards(): (merged_down / jnp.expand_dims(scale_down, 2)).astype(jnp.bfloat16)]
    convert_element_type x1 -> x0, local copies, waits for them, and re-layouts: 33.4 us -> none  [shards(): (merged_down / jnp.expand_dims(scale_down, 2)).astype(jnp.bfloat16)]
    reduce_sum x1 -> x0, other arithmetic: 24.2 us -> none  [shards(): total_down = lax.psum(jnp.sum(merged_down * merged_down, axis=2), 'fsdp')]
    unnamed x7 -> x6, local copies, waits for them, and re-layouts: 4.74 us -> 20 us
  transfers between devices with their start and end apart: 2 -> 0, of which waited for: 1 -> 0; matrix products, arithmetic and copies ran while one was open for 0% -> 0% of each run, Pallas kernels for 0% -> 0%
where the time goes in v1:
time: 612 us
  Pallas kernels  590 us (96%)
  local copies, waits for them, and re-layouts  20.7 us (3%)
    pallas_call x1, Pallas kernels, step(): pl.pallas_call(functools.partial(kernel, dims), out_shape=(jax.ShapeDtype...  590 us
    unnamed x6, local copies, waits for them, and re-layouts  20 us

profile of v1, /device:TPU:0, one launch (start us, length us, event | category | flops | bytes accessed | tf_op | source)
XLA Modules:
  0.0 611.6 jit_solution(856490335137560918)
XLA Ops:
  0.6 0.0 copy-start
  0.6 0.7 copy-done
  1.3 0.0 copy-start.1
  1.3 0.7 copy-done.1
  2.0 590.2 %shard_map.67 = (bf16[4,800,4096]{2,1,0:T(8,128)(2,1)}, f32[20,2,128]{2,1,0:T(2,128)S(1)}, bf16[4,8,4,512]{3,2,1,0:T(4,128)(2,1)S(1)}) custom-call(f32[4,8,800,512]{3,2,1,0:T(8,128)} %bitcast.15, bf16[4,8,800,512]{3,2,1,0:T(8,128)(2,1)} %bitcast.16, f32[4,512]{1,0:T(4,128)S(1)} %bitcast.13, f32[1,512]{1,0:T(1,128)S(1)} %bitcast.14), custom_call_target="tpu_custom_call" | custom-call | tf_op jit(solution)/shard_map/pallas_call | solution.py:203
  592.3 0.7 reshape.20
  593.0 0.7 copy.8
  593.7 17.9 %copy.10 = bf16[4,800,4096]{2,1,0:T(8,128)(2,1)} copy(bf16[4,800,4096]{2,1,0:T(8,128)(2,1)} %get-tuple-element.12) | data formatting | bytes 52428800
  (1 shorter events, 0.0 us)
Async XLA Ops:
  0.6 0.7 copy-start
  1.3 0.7 copy-start.1
